TPU v7x, 128 devices: a whole 4x4x4 slice. The times are simulated.
128 devices in a mesh: member: 32 (over x, y, core), lat: 4 (over z).
Axes of the slice: x: 4, y: 4, z: 4, core: 2. Of those that a mesh axis runs over, the one named last changes fastest.
Arguments:
- ensemble: float32 [64, 3, 1, 128, 1440], P('member', None, None, 'lat'), may hold values from -6 to 6
- observation: float32 [3, 1, 128, 1440], P(None, None, 'lat'), may hold values from -6 to 6
- valid_mask: int32 [64], P('member'), may hold values from 0 to 1, as said below
- band_start: int32 [4], P('lat'), may hold values from 0 to 689
Outputs:
- crps_field: float32 [3, 1, 128, 1440], P(None, None, ('lat', 'member'))
- score_table: float32 [3, 1], replicated
Inputs may be any that keep to these rules, and one draw needn't show every extreme that they name: `valid_mask`: exactly 50 entries are 1, at positions drawn afresh.
All inputs are finite; a program needn't handle non-finite values.
Results may differ from a plain program's by a relative error of at most 0.0001.
Values sent between devices are 32-bit elements; how exact they have to be, the bound alone decides.
A program may use at most 64 MiB of HBM per device.

v0:
```python
import functools
import math

import jax
import jax.numpy as jnp
from jax import lax
from jax.sharding import Mesh
from jax.sharding import PartitionSpec as P

GRID_LAT = 721
GRID_LON = 1440
MEMBER = ("member_0", "member_1", "member_2")
MEMBER_LAT = ("member_0", "member_1", "member_2", "lat")
LAT_MEMBER = ("lat", "member_0", "member_1", "member_2")


def sent_to_all(x, axis):
    copies = jnp.broadcast_to(x, (lax.axis_size(axis), *x.shape))
    return lax.all_to_all(copies, axis, split_axis=0, concat_axis=0, tiled=True)


def laid_out(parts, dim):
    parts = jnp.moveaxis(parts, 0, dim)
    dims = parts.shape
    return parts.reshape(*dims[:dim], dims[dim] * dims[dim + 1], *dims[dim + 2 :])


def collect(x, axis, dim):
    parts = sent_to_all(x, axis)
    return laid_out(parts, dim)


def by_axis(x, axes):
    return functools.reduce(lax.psum, axes, x)


def on_device(ensemble, observation, valid_mask, band_start):
    member_flags = valid_mask.astype(jnp.float32)
    lat_rows = ensemble.shape[3]
    block_rows = lat_rows // lax.axis_size(MEMBER)
    row_offset = lax.axis_index(MEMBER) * block_rows
    members = lax.all_to_all(ensemble, MEMBER, split_axis=3, concat_axis=0, tiled=True)
    all_flags = collect(member_flags, MEMBER, 0)
    slot_total = members.shape[0]
    truth_slice = lax.dynamic_slice_in_dim(observation, row_offset, block_rows, 2)
    valid_count = jnp.sum(all_flags)
    flag_column = all_flags[:, None, None, None, None]
    skill_term = jnp.sum(flag_column * jnp.abs(members - truth_slice[None]), axis=0)
    group_count = slot_total // 8
    blocks = members.reshape((group_count, 8) + members.shape[1:])
    block_flags = all_flags.reshape(group_count, 8)

    def block_sum(block_item):
        block_slab, flags_here = block_item

        def add_one(position, running_sum):
            one_slab = lax.dynamic_index_in_dim(block_slab, position, 0, keepdims=True)
            one_flag = lax.dynamic_index_in_dim(flags_here, position, 0, keepdims=False)
            return running_sum + one_flag * jnp.sum(
                flag_column * jnp.abs(one_slab - members), axis=0
            )

        return lax.fori_loop(0, 8, add_one, jnp.zeros(truth_slice.shape, jnp.float32))

    spread = jnp.sum(lax.map(block_sum, (blocks, block_flags)), axis=0)
    crps_field = skill_term / valid_count - spread / (2.0 * valid_count * (valid_count - 1.0))
    row_index = (band_start[0] + row_offset + jnp.arange(block_rows, dtype=jnp.int32)).astype(
        jnp.float32
    )
    weight = jnp.cos((90.0 - row_index * 180.0 / (GRID_LAT - 1)) * math.pi / 180.0)
    partial_sums = jnp.sum(crps_field * weight[:, None], axis=(2, 3))
    totals = by_axis(partial_sums, MEMBER_LAT)
    score_table = totals / (lax.axis_size("lat") * lat_rows * GRID_LON)
    return (crps_field, score_table)


def solution(mesh):
    torus = Mesh(
        mesh.devices.reshape(4, 4, 2, mesh.shape["lat"]),
        ("member_0", "member_1", "member_2", "lat"),
    )
    in_specs = (P(MEMBER, None, None, "lat", None), P(None, None, "lat", None), P(MEMBER), P("lat"))
    out_specs = (P(None, None, LAT_MEMBER, None), P())
    return jax.shard_map(
        on_device, mesh=torus, in_specs=in_specs, out_specs=out_specs, check_vma=False
    )
```

profile of v0, /device:TPU:1, one launch (start us, length us, event | category | flops | bytes accessed | tf_op | source)
XLA Modules:
  0.0 281.1 jit_solution(1610681111426072009)
XLA Ops:
  2.0 8.6 %all-to-all-start = ((f32[32,1,2]{2,1,0:T(1,128)}), f32[32,1,2]{2,1,0:T(1,128)S(1)}, u32[]{:S(2)}, u32[]{:S(2)}) async-start(f32[32,1,2]{2,1,0:T(1,128)} %broadcast_in_dim.11), calls=%async_computation | async-start | bytes 32768 | tf_op jit(solution)/shard_map/all_to_all | solution.py:19
  10.6 3.2 %copy.28 = f32[2,3,1,32,1440]{4,1,2,0,3:T(4,128)} copy(f32[2,3,1,32,1440]{4,3,2,1,0:T(8,128)} %param.8) | data formatting | bytes 2211840 | tf_op args[0]
  13.8 3.7 %all-to-all-done = f32[32,1,2]{2,1,0:T(1,128)S(1)} async-done(((f32[32,1,2]{2,1,0:T(1,128)}), f32[32,1,2]{2,1,0:T(1,128)S(1)}, u32[]{:S(2)}, u32[]{:S(2)}) %all-to-all-start) | async-done | bytes 288 | tf_op jit(solution)/shard_map/all_to_all | solution.py:19
  17.5 4.3 %all-to-all-start.1 = ((f32[2,3,1,32,1440]{4,1,2,0,3:T(4,128)}), f32[2,3,1,32,1440]{4,1,2,0,3:T(4,128)S(1)}, u32[]{:S(2)}, u32[]{:S(2)}) async-start(f32[2,3,1,32,1440]{4,1,2,0,3:T(4,128)} %copy.28), calls=%async_computation.1 | async-start | bytes 3145728 | tf_op jit(solution)/shard_map/all_to_all | solution.py:42
  25.9 18.6 %all-to-all-done.1 = f32[2,3,1,32,1440]{4,1,2,0,3:T(4,128)S(1)} async-done(((f32[2,3,1,32,1440]{4,1,2,0,3:T(4,128)}), f32[2,3,1,32,1440]{4,1,2,0,3:T(4,128)S(1)}, u32[]{:S(2)}, u32[]{:S(2)}) %all-to-all-start.1) | async-done | bytes 1105952 | tf_op jit(solution)/shard_map/all_to_all | solution.py:42
  46.5 202.5 %while.25 = (s32[]{:T(128)}, f32[8,3,1,1,1440]{4,3,2,1,0:T(1,128)S(1)}, f32[8,8,3,1,1,1440]{5,4,3,2,1,0:T(1,128)S(1)}, f32[8,8]{1,0:T(8,128)S(1)}, f32[64,1,1,1,...) while((s32[]{:T(128)}, ...), condition=%wide.region_6.7_spmd, body=%wide.region_2.6_spmd.sunk | while | flops 1114565 | bytes 1609964 | solution.py:65
  46.6 25.2 %while.26 = (s32[]{:T(128)}, f32[3,1,1,1440]{3,2,1,0:T(1,128)S(1)}, f32[8]{0:T(128)S(1)}, f32[64,1,1,1,1]{0,4,3,2,1:T(1,128)S(1)}, f32[8,3,1,1,1440]{4,3,2,1,0:T...) while((s32[]{:T(128)}, f32[3,1,1,1440]{3,2,1,0:T(1,128)S(1)}, ...), condition=%wide.region_5.5_spmd.clone, body=%wide.region_3.4_spmd.clone.sunk | while | flops 1114563 | bytes 1296371 | solution.py:63
  52.9 1.7 multiply_reduce_fusion.4
  62.4 1.7 multiply_reduce_fusion.4
  65.6 1.7 multiply_reduce_fusion.4
  71.9 25.2 %while.26 = (s32[]{:T(128)}, f32[3,1,1,1440]{3,2,1,0:T(1,128)S(1)}, f32[8]{0:T(128)S(1)}, f32[64,1,1,1,1]{0,4,3,2,1:T(1,128)S(1)}, f32[8,3,1,1,1440]{4,3,2,1,0:T...) while((s32[]{:T(128)}, f32[3,1,1,1440]{3,2,1,0:T(1,128)S(1)}, ...), condition=%wide.region_5.5_spmd.clone, body=%wide.region_3.4_spmd.clone.sunk | while | flops 1114563 | bytes 1296371 | solution.py:63
  75.1 1.7 multiply_reduce_fusion.4
  78.3 1.7 multiply_reduce_fusion.4
  87.7 1.7 multiply_reduce_fusion.4
  97.2 25.2 %while.26 = (s32[]{:T(128)}, f32[3,1,1,1440]{3,2,1,0:T(1,128)S(1)}, f32[8]{0:T(128)S(1)}, f32[64,1,1,1,1]{0,4,3,2,1:T(1,128)S(1)}, f32[8,3,1,1,1440]{4,3,2,1,0:T...) while((s32[]{:T(128)}, f32[3,1,1,1440]{3,2,1,0:T(1,128)S(1)}, ...), condition=%wide.region_5.5_spmd.clone, body=%wide.region_3.4_spmd.clone.sunk | while | flops 1114563 | bytes 1296371 | solution.py:63
  122.5 25.2 %while.26 = (s32[]{:T(128)}, f32[3,1,1,1440]{3,2,1,0:T(1,128)S(1)}, f32[8]{0:T(128)S(1)}, f32[64,1,1,1,1]{0,4,3,2,1:T(1,128)S(1)}, f32[8,3,1,1,1440]{4,3,2,1,0:T...) while((s32[]{:T(128)}, f32[3,1,1,1440]{3,2,1,0:T(1,128)S(1)}, ...), condition=%wide.region_5.5_spmd.clone, body=%wide.region_3.4_spmd.clone.sunk | while | flops 1114563 | bytes 1296371 | solution.py:63
  147.9 25.2 %while.26 = (s32[]{:T(128)}, f32[3,1,1,1440]{3,2,1,0:T(1,128)S(1)}, f32[8]{0:T(128)S(1)}, f32[64,1,1,1,1]{0,4,3,2,1:T(1,128)S(1)}, f32[8,3,1,1,1440]{4,3,2,1,0:T...) while((s32[]{:T(128)}, f32[3,1,1,1440]{3,2,1,0:T(1,128)S(1)}, ...), condition=%wide.region_5.5_spmd.clone, body=%wide.region_3.4_spmd.clone.sunk | while | flops 1114563 | bytes 1296371 | solution.py:63
  173.2 25.2 %while.26 = (s32[]{:T(128)}, f32[3,1,1,1440]{3,2,1,0:T(1,128)S(1)}, f32[8]{0:T(128)S(1)}, f32[64,1,1,1,1]{0,4,3,2,1:T(1,128)S(1)}, f32[8,3,1,1,1440]{4,3,2,1,0:T...) while((s32[]{:T(128)}, f32[3,1,1,1440]{3,2,1,0:T(1,128)S(1)}, ...), condition=%wide.region_5.5_spmd.clone, body=%wide.region_3.4_spmd.clone.sunk | while | flops 1114563 | bytes 1296371 | solution.py:63
  198.5 25.2 %while.26 = (s32[]{:T(128)}, f32[3,1,1,1440]{3,2,1,0:T(1,128)S(1)}, f32[8]{0:T(128)S(1)}, f32[64,1,1,1,1]{0,4,3,2,1:T(1,128)S(1)}, f32[8,3,1,1,1440]{4,3,2,1,0:T...) while((s32[]{:T(128)}, f32[3,1,1,1440]{3,2,1,0:T(1,128)S(1)}, ...), condition=%wide.region_5.5_spmd.clone, body=%wide.region_3.4_spmd.clone.sunk | while | flops 1114563 | bytes 1296371 | solution.py:63
  223.8 25.2 %while.26 = (s32[]{:T(128)}, f32[3,1,1,1440]{3,2,1,0:T(1,128)S(1)}, f32[8]{0:T(128)S(1)}, f32[64,1,1,1,1]{0,4,3,2,1:T(1,128)S(1)}, f32[8,3,1,1,1440]{4,3,2,1,0:T...) while((s32[]{:T(128)}, f32[3,1,1,1440]{3,2,1,0:T(1,128)S(1)}, ...), condition=%wide.region_5.5_spmd.clone, body=%wide.region_3.4_spmd.clone.sunk | while | flops 1114563 | bytes 1296371 | solution.py:63
  250.0 6.6 %psum.28 = f32[3,1]{0,1:T(1,128)S(1)} all-reduce(f32[3,1]{0,1:T(1,128)S(1)} %bitcast.51), channel_id=1, replica_groups=mesh['member_0'=4,'member_1'=4,'member_2'=2,'lat'=4] {'member_0'}, use_global_device_ids=true, to_apply=%region_9.10 | all-reduce | flops 3 | bytes 24 | tf_op jit(solution)/shard_map/psum | solution.py:34
  256.6 7.2 %psum.29 = f32[3,1]{0,1:T(1,128)S(1)} all-reduce(f32[3,1]{0,1:T(1,128)S(1)} %psum.28), channel_id=1, replica_groups=mesh['member_0'=4,'member_1'=4,'member_2'=2,'lat'=4] {'member_1'}, use_global_device_ids=true, to_apply=%region_10.11 | all-reduce | flops 3 | bytes 24 | tf_op jit(solution)/shard_map/psum | solution.py:34
  263.7 6.5 %psum.30 = f32[3,1]{0,1:T(1,128)S(1)} all-reduce(f32[3,1]{0,1:T(1,128)S(1)} %psum.29), channel_id=1, replica_groups=mesh['member_0'=4,'member_1'=4,'member_2'=2,'lat'=4] {'member_2'}, use_global_device_ids=true, to_apply=%region_11.12 | all-reduce | flops 3 | bytes 24 | tf_op jit(solution)/shard_map/psum | solution.py:34
  270.8 9.7 %psum.31 = f32[3,1]{0,1:T(1,128)S(1)} all-reduce(f32[3,1]{0,1:T(1,128)S(1)} %psum.30), channel_id=1, replica_groups=mesh['member_0'=4,'member_1'=4,'member_2'=2,'lat'=4] {'lat'}, use_global_device_ids=true, to_apply=%region_12.13 | all-reduce | flops 3 | bytes 24 | tf_op jit(solution)/shard_map/psum | solution.py:34
  (428 shorter events, 197.0 us)
Async XLA Ops:
  0.6 21.1 %copy-start = (f32[3,1,32,1440]{3,2,1,0:T(8,128)S(1)}, f32[3,1,32,1440]{3,2,1,0:T(8,128)}, u32[]{:S(2)}) copy-start(f32[3,1,32,1440]{3,2,1,0:T(8,128)} %param.9) | copy-start | bytes 1658884
  2.0 15.5 %all-to-all-start = ((f32[32,1,2]{2,1,0:T(1,128)}), f32[32,1,2]{2,1,0:T(1,128)S(1)}, u32[]{:S(2)}, u32[]{:S(2)}) async-start(f32[32,1,2]{2,1,0:T(1,128)} %broadcast_in_dim.11), calls=%async_computation | async-start | bytes 32768 | tf_op jit(solution)/shard_map/all_to_all | solution.py:19
  17.5 27.0 %all-to-all-start.1 = ((f32[2,3,1,32,1440]{4,1,2,0,3:T(4,128)}), f32[2,3,1,32,1440]{4,1,2,0,3:T(4,128)S(1)}, u32[]{:S(2)}, u32[]{:S(2)}) async-start(f32[2,3,1,32,1440]{4,1,2,0,3:T(4,128)} %copy.28), calls=%async_computation.1 | async-start | bytes 3145728 | tf_op jit(solution)/shard_map/all_to_all | solution.py:42
where the time goes:
time: 283 us; the launch traced here: 281 us
  other arithmetic  160 us (57%)
  local copies, waits for them, and re-layouts  50.6 us (18%)
  blocking collectives  29.9 us (11%)
  waiting for transfers between devices  22.2 us (8%)
  starting transfers between devices  12.9 us (5%)
  loops' own time  2.88 us (1%)
    reduce_sum x64, other arithmetic, add_one(): jnp.sum(flag_column * jnp.abs(one_slab - members), axis=0)  108 us
    mul x64, other arithmetic, add_one(): one_flag * jnp.sum(flag_column * jnp.abs(one_slab - members), axis=0)  44.4 us
    dynamic_slice x64, local copies, waits for them, and re-layouts, add_one(): one_flag = lax.dynamic_index_in_dim(flags_here, position, 0, keepdims=False)  42.6 us
    psum x4, blocking collectives, by_axis(): return functools.reduce(lax.psum, axes, x)  29.9 us
    all_to_all x1, waiting for transfers between devices, on_device(): lax.all_to_all(ensemble, MEMBER, split_axis=3, concat_axis=0, tiled=True)  18.6 us
    all_to_all x1, starting transfers between devices, sent_to_all(): return lax.all_to_all(copies, axis, split_axis=0, concat_axis=0, tiled=True)  8.58 us
  transfers between devices with their start and end apart: 2, of which 2 were waited for; matrix products, arithmetic and copies ran while one was open for 2% of the time, Pallas kernels for 0%

commit v1 on v0

v1 whole, which is shorter than its diff:
```python
import functools
import math

import jax
import jax.numpy as jnp
from jax import lax
from jax.experimental import pallas as pl
from jax.experimental.pallas import tpu as pltpu
from jax.sharding import Mesh
from jax.sharding import PartitionSpec as P

GRID_LAT = 721
GRID_LON = 1440
VALID = 50
BIG = 1.0e30
MEMBER = ("member_0", "member_1", "member_2")
LAT_MEMBER = ("lat", "member_0", "member_1", "member_2")
AXES = ("member_0", "member_1", "member_2", "lat")
SIZES = {"member_0": 4, "member_1": 4, "member_2": 2, "lat": 4}
MESH_ID = pl.DeviceIdType.MESH

LANES = 128
VARS = 3
FULL = GRID_LON // LANES
TAIL = GRID_LON - FULL * LANES
ROWS = VARS * FULL + 1
SENT = 2 * ROWS
S_STRIDE = 72
R_STRIDE = 80
COLS = 5


def offsets(axes):
    found = [{}]
    for axis in axes:
        found = [dict(o, **{axis: k}) for o in found for k in range(SIZES[axis])]
    found = [o for o in found if any(o.values())]

    def hops(o):
        return sum(min(k, SIZES[a] - k) if a != "member_2" else 0.3 * k for a, k in o.items())

    return sorted(found, key=lambda o: -hops(o))


def peer(offset):
    return {a: lax.rem(lax.axis_index(a) + offset.get(a, 0), SIZES[a]) for a in AXES}


def member_of(coords):
    return (coords["member_0"] * 4 + coords["member_1"]) * 2 + coords["member_2"]


def merge_pairs(lo, n, step, out):
    jump = step * 2
    if jump < n:
        merge_pairs(lo, n, jump, out)
        merge_pairs(lo + step, n, jump, out)
        out.extend((i, i + step) for i in range(lo + step, lo + n - step, jump))
    else:
        out.append((lo, lo + step))


def sort_pairs(lo, n, out):
    if n > 2:
        half = n // 2
        sort_pairs(lo, half, out)
        sort_pairs(lo + half, half, out)
        merge_pairs(lo, n, 1, out)


def pruned(pairs, keep):
    needed = set(range(keep))
    kept = []
    for i, j in reversed(pairs):
        if i in needed or j in needed:
            kept.append((i, j, i in needed, j in needed))
            needed |= {i, j}
    return kept[::-1]


def kernel(
    ens, obs, mask, band, crps_out, score_out,
    xv, ov, sbuf, rbuf, obuf, cbuf, asend, abuf,
    load_sem, obs_sem, send_sem, recv_sem, asend_sem, arecv_sem, ready_sem,
):
    plane = offsets(MEMBER)
    line = offsets(("lat",))
    everyone = offsets(AXES)
    here = {a: lax.axis_index(a) for a in AXES}
    me = member_of(here)

    barrier = pltpu.get_barrier_semaphore()
    for off in plane + line:
        pl.semaphore_signal(barrier, inc=1, device_id=peer(off), device_id_type=MESH_ID)

    load = pltpu.make_async_copy(ens.at[:, :, 0], xv, load_sem)
    load.start()
    tile_row = pl.multiple_of((me // 8) * 8, 8)
    obs_load = pltpu.make_async_copy(obs.at[:, 0, pl.ds(tile_row, 8)], ov, obs_sem)
    obs_load.start()

    flags = [mask[m].astype(jnp.float32) for m in range(2)]
    fills = [(1.0 - f) * BIG for f in flags]
    lane = lax.broadcasted_iota(jnp.int32, (8, LANES), 1)
    load.wait()
    for t in range(4):
        rows = pl.ds(8 * t, 8)

        def put(row, low, high):
            start = 8 * t * S_STRIDE + 2 * row
            sbuf[pl.ds(start, 8, stride=S_STRIDE), :] = low
            sbuf[pl.ds(start + 1, 8, stride=S_STRIDE), :] = high

        tails = []
        for v in range(VARS):
            for c in range(FULL + 1):
                width = LANES if c < FULL else TAIL
                pair = [
                    xv[m, v, rows, pl.ds(c * LANES, width)] * flags[m] + fills[m] for m in range(2)
                ]
                low, high = jnp.minimum(*pair), jnp.maximum(*pair)
                if c < FULL:
                    put(v * FULL + c, low, high)
                else:
                    tails.append((low, high))
        rest = jnp.zeros((8, LANES - VARS * TAIL), jnp.float32)
        put(
            VARS * FULL,
            jnp.concatenate([p[0] for p in tails] + [rest], axis=1),
            jnp.concatenate([p[1] for p in tails] + [rest], axis=1),
        )

    pl.semaphore_wait(barrier, len(plane) + len(line))
    for off in line:
        pl.semaphore_signal(ready_sem, inc=1, device_id=peer(off), device_id_type=MESH_ID)

    copies = []
    for i, off in enumerate(plane):
        target = peer(off)
        start = pl.multiple_of(member_of(target) * S_STRIDE, 8)
        copy = pltpu.make_async_remote_copy(
            src_ref=sbuf.at[pl.ds(start, SENT)],
            dst_ref=rbuf.at[pl.ds(i * R_STRIDE, SENT)],
            send_sem=send_sem,
            recv_sem=recv_sem.at[i],
            device_id=target,
            device_id_type=MESH_ID,
        )
        copy.start()
        copies.append(copy)

    own = pl.multiple_of(me * S_STRIDE, 8)
    rbuf[pl.ds(31 * R_STRIDE, S_STRIDE), :] = sbuf[pl.ds(own, S_STRIDE), :]
    obs_load.wait()
    sub = lax.broadcasted_iota(jnp.int32, (8, LANES), 0)
    chosen = sub == lax.rem(me, 8)
    obs_tails = []
    for v in range(VARS):
        for c in range(FULL):
            part = jnp.where(chosen, ov[v, :, pl.ds(c * LANES, LANES)], 0.0)
            obuf[pl.ds(v * FULL + c, 1), :] = jnp.sum(part, axis=0, keepdims=True)
        part = jnp.where(chosen[:, :TAIL], ov[v, :, pl.ds(FULL * LANES, TAIL)], 0.0)
        obs_tails.append(jnp.sum(part, axis=0, keepdims=True))
    rest = jnp.zeros((1, LANES - VARS * TAIL), jnp.float32)
    obuf[pl.ds(VARS * FULL, 1), :] = jnp.concatenate(obs_tails + [rest], axis=1)
    global_row = (band[0] + me).astype(jnp.float32)
    angle = (90.0 - jnp.full((1, LANES), global_row) * 180.0 / (GRID_LAT - 1)) * math.pi / 180.0
    weight = jnp.cos(angle)

    for copy in copies:
        copy.wait_recv()

    pairs = []
    sort_pairs(0, 64, pairs)
    pairs = pruned(pairs, VALID)

    def column(q, sums):
        vals = [
            rbuf[pl.ds((k // 2) * R_STRIDE + 16 * q + k % 2, 8, stride=2), :] for k in range(64)
        ]
        for i, j, want_low, want_high in pairs:
            a, b = vals[i], vals[j]
            vals[i] = jnp.minimum(a, b) if want_low else None
            vals[j] = jnp.maximum(a, b) if want_high else None
        truth = obuf[pl.ds(pl.multiple_of(8 * q, 8), 8), :]
        skill = [jnp.zeros((8, LANES), jnp.float32) for _ in range(2)]
        spread = [jnp.zeros((8, LANES), jnp.float32) for _ in range(2)]
        for k in range(VALID // 2):
            low, high = vals[k], vals[VALID - 1 - k]
            skill[0] = skill[0] + jnp.abs(low - truth)
            skill[1] = skill[1] + jnp.abs(high - truth)
            spread[k % 2] = spread[k % 2] + (high - low) * float(VALID - 1 - 2 * k)
        crps = (skill[0] + skill[1]) * (1.0 / VALID) - (spread[0] + spread[1]) * (
            1.0 / (VALID * (VALID - 1.0))
        )
        cbuf[pl.ds(pl.multiple_of(8 * q, 8), 8), :] = crps
        row = sub + 8 * q
        result = []
        for v in range(VARS):
            inside = (row >= v * FULL) & (row < (v + 1) * FULL)
            in_tail = (row == VARS * FULL) & (lane >= v * TAIL) & (lane < (v + 1) * TAIL)
            result.append(sums[v] + jnp.where(inside | in_tail, crps, 0.0))
        return tuple(result)

    sums = lax.fori_loop(
        0, COLS, column, tuple(jnp.zeros((8, LANES), jnp.float32) for _ in range(VARS))
    )
    totals = [jnp.sum(s, axis=(0, 1), keepdims=True) for s in sums]
    one_lane = lax.broadcasted_iota(jnp.int32, (1, LANES), 1)
    message = jnp.zeros((1, LANES), jnp.float32)
    for v in range(VARS):
        message = jnp.where(one_lane == v, totals[v] * weight, message)
    my_id = here["lat"] * 32 + me
    asend[0] = message
    abuf[my_id] = message

    pl.semaphore_wait(ready_sem, len(line))
    for off in everyone:
        pltpu.make_async_remote_copy(
            src_ref=asend.at[0],
            dst_ref=abuf.at[my_id],
            send_sem=asend_sem,
            recv_sem=arecv_sem,
            device_id=peer(off),
            device_id_type=MESH_ID,
        ).start()

    for v in range(VARS):
        for c in range(FULL):
            crps_out[v, 0, :, pl.ds(c * LANES, LANES)] = cbuf[pl.ds(v * FULL + c, 1), :]
        last = cbuf[pl.ds(VARS * FULL, 1), :]
        crps_out[v, 0, :, pl.ds(FULL * LANES, TAIL)] = last[:, v * TAIL : (v + 1) * TAIL]

    sent = sbuf.at[pl.ds(0, len(plane) * SENT)]
    pltpu.make_async_copy(sent, sent, send_sem).wait()
    arrived = abuf.at[pl.ds(0, len(everyone))]
    pltpu.make_async_copy(arrived, arrived, arecv_sem).wait()
    total = jnp.sum(abuf[:, 0, :], axis=0, keepdims=True) * (1.0 / (4 * 32 * GRID_LON))
    score_out[...] = total
    pltpu.make_async_copy(arrived, arrived, asend_sem).wait()


def on_device(ensemble, observation, valid_mask, band_start):
    vmem = pl.BlockSpec(memory_space=pltpu.VMEM)
    smem = pl.BlockSpec(memory_space=pltpu.SMEM)
    hbm = pl.BlockSpec(memory_space=pl.ANY)
    crps_field, score = pl.pallas_call(
        kernel,
        out_shape=(
            jax.ShapeDtypeStruct((VARS, 1, 1, GRID_LON), jnp.float32),
            jax.ShapeDtypeStruct((1, LANES), jnp.float32),
        ),
        in_specs=[hbm, hbm, smem, smem],
        out_specs=(vmem, vmem),
        scratch_shapes=[
            pltpu.VMEM((2, VARS, 32, GRID_LON), jnp.float32),
            pltpu.VMEM((VARS, 8, GRID_LON), jnp.float32),
            pltpu.VMEM((32 * S_STRIDE, LANES), jnp.float32),
            pltpu.VMEM((32 * R_STRIDE, LANES), jnp.float32),
            pltpu.VMEM((8 * COLS, LANES), jnp.float32),
            pltpu.VMEM((8 * COLS, LANES), jnp.float32),
            pltpu.VMEM((1, 1, LANES), jnp.float32),
            pltpu.VMEM((128, 1, LANES), jnp.float32),
            pltpu.SemaphoreType.DMA,
            pltpu.SemaphoreType.DMA,
            pltpu.SemaphoreType.DMA,
            pltpu.SemaphoreType.DMA((31,)),
            pltpu.SemaphoreType.DMA,
            pltpu.SemaphoreType.DMA,
            pltpu.SemaphoreType.REGULAR,
        ],
        compiler_params=pltpu.CompilerParams(collective_id=0, has_side_effects=True),
        name="crps",
    )(ensemble, observation, valid_mask, band_start)
    return crps_field, score[0, :VARS].reshape(VARS, 1)


def solution(mesh):
    torus = Mesh(
        mesh.devices.reshape(4, 4, 2, mesh.shape["lat"]),
        ("member_0", "member_1", "member_2", "lat"),
    )
    in_specs = (P(MEMBER, None, None, "lat", None), P(None, None, "lat", None), P(MEMBER), P("lat"))
    out_specs = (P(None, None, LAT_MEMBER, None), P())
    return jax.shard_map(
        on_device, mesh=torus, in_specs=in_specs, out_specs=out_specs, check_vma=False
    )
```

time: 283 us -> 35.4 us (0.13)
  other arithmetic: 160 us -> 0 us
  local copies, waits for them, and re-layouts: 50.6 us -> 2.51 us
  Pallas kernels: 0 us -> 31.4 us
  blocking collectives: 29.9 us -> 0 us
  waiting for transfers between devices: 22.2 us -> 0 us
  starting transfers between devices: 12.9 us -> 0 us
  loops' own time: 2.88 us -> 0 us
    reduce_sum x68 -> x0, other arithmetic: 111 us -> none  [the longest x64 108 us: add_one(): jnp.sum(flag_column * jnp.abs(one_slab - members), axis=0)]
    mul x64 -> x0, other arithmetic: 44.4 us -> none  [add_one(): one_flag * jnp.sum(flag_column * jnp.abs(one_slab - members), axis=0)]
    dynamic_slice x129 -> x0, local copies, waits for them, and re-layouts: 43.2 us -> none  [the longest x64 42.6 us: add_one(): one_flag = lax.dynamic_index_in_dim(flags_here, position, 0, keepdims=False)]
    pallas_call x0 -> x1, Pallas kernels: none -> 31.4 us  [on_device(): pl.pallas_call(kernel, out_shape=(jax.ShapeDtypeStruct((VARS, 1, 1, GRID_...]
    psum x4 -> x0, blocking collectives: 29.9 us -> none  [by_axis(): return functools.reduce(lax.psum, axes, x)]
    all_to_all x2 -> x0, waiting for transfers between devices: 22.2 us -> none  [the longest x1 18.6 us: on_device(): lax.all_to_all(ensemble, MEMBER, split_axis=3, concat_axis=0, tiled=True)]
    all_to_all x2 -> x0, starting transfers between devices: 12.9 us -> none  [the longest x1 8.58 us: sent_to_all(): return lax.all_to_all(copies, axis, split_axis=0, concat_axis=0, tiled=True)]
    add x64 -> x0, other arithmetic: 3.03 us -> none  [add_one(): running_sum + one_flag * jnp.sum(flag_column * jnp.abs(one_slab - members...]
  transfers between devices with their start and end apart: 2 -> 0, of which waited for: 2 -> 0; matrix products, arithmetic and copies ran while one was open for 2% -> 0% of each run, Pallas kernels for 0% -> 0%
where the time goes in v1:
time: 35.4 us; the launch traced here: 35.2 us
  Pallas kernels  31.4 us (89%)
  local copies, waits for them, and re-layouts  2.51 us (7%)
  between operations  1.29 us (4%)
    pallas_call x1, Pallas kernels, on_device(): pl.pallas_call(kernel, out_shape=(jax.ShapeDtypeStruct((VARS, 1, 1, GRID_...  31.4 us
    unnamed x1, local copies, waits for them, and re-layouts  1.33 us
    another operation x1, local copies, waits for them, and re-layouts, on_device(): return (crps_field, score[0, :VARS].reshape(VARS, 1))  1.18 us

profile of v1, /device:TPU:1, one launch (start us, length us, event | category | flops | bytes accessed | tf_op | source)
XLA Modules:
  0.0 35.2 jit_solution(12362136752448368373)
XLA Ops:
  1.3 31.4 %crps.1 = (f32[3,1,1,1440]{3,2,1,0:T(1,128)}, f32[1,128]{1,0:T(1,128)}) custom-call(f32[2,3,1,32,1440]{4,3,2,1,0:T(8,128)} %ens.1, f32[3,1,32,1440]{3,2,1,0:T(8,128)} %obs.1, s32[2]{0:T(128)} %mask.1, s32[1]{0:T(128)S(6)} %copy.7.band), custom_call_target="tpu_custom_call" | custom-call | tf_op jit(solution)/shard_map/crps/pallas_call | solution.py:247
  32.7 1.2 %slice_bitcast_fusion = f32[3,1]{0,1:T(1,128)} fusion(f32[1,128]{1,0:T(1,128)} %get-tuple-element.5), kind=kLoop, calls=%fused_computation | loop fusion | bytes 24 | tf_op jit(solution)/shard_map/reshape;squeeze | solution.py:275
  33.9 1.3 %copy.8 = f32[3,1,1,1440]{3,2,1,0:T(1,128)} copy(f32[3,1,1,1440]{3,2,1,0:T(1,128)} %get-tuple-element.8) | data formatting | bytes 34560

commit v2 on v1

--- a/solution.py
+++ b/solution.py
@@ -78,36 +78,56 @@
     return kept[::-1]
 
 
+BLOCKS = (2, 1, 3, 0)
+PLANE = [[o for o in offsets(MEMBER) if o["member_0"] == dx] for dx in BLOCKS]
+LINE = offsets(("lat",))
+EVERYONE = offsets(AXES)
+
+
+def sort_into(vals, pairs):
+    for i, j, want_low, want_high in pairs:
+        a, b = vals[i], vals[j]
+        vals[i] = jnp.minimum(a, b) if want_low else None
+        vals[j] = jnp.maximum(a, b) if want_high else None
+
+
 def kernel(
     ens, obs, mask, band, crps_out, score_out,
-    xv, ov, sbuf, rbuf, obuf, cbuf, asend, abuf,
-    load_sem, obs_sem, send_sem, recv_sem, asend_sem, arecv_sem, ready_sem,
+    xv, ov, sbuf, rbuf, obuf, cbuf, asend, abuf, mask_s,
+    load_sem, obs_sem, flag_sem, send_sem, recv_sem, asend_sem, arecv_sem, ready_sem,
 ):
-    plane = offsets(MEMBER)
-    line = offsets(("lat",))
-    everyone = offsets(AXES)
     here = {a: lax.axis_index(a) for a in AXES}
     me = member_of(here)
 
+    mask_load = pltpu.make_async_copy(mask, mask_s, flag_sem)
+    mask_load.start()
+    loads = []
+    for k, dx in enumerate(BLOCKS):
+        first = pl.multiple_of(lax.rem(here["member_0"] + dx, 4) * 8, 8)
+        load = pltpu.make_async_copy(ens.at[:, :, 0, pl.ds(first, 8)], xv.at[k], load_sem.at[k])
+        load.start()
+        loads.append(load)
+
     barrier = pltpu.get_barrier_semaphore()
-    for off in plane + line:
+    plane = [o for block in PLANE for o in block]
+    for off in offsets(MEMBER) + LINE:
         pl.semaphore_signal(barrier, inc=1, device_id=peer(off), device_id_type=MESH_ID)
 
-    load = pltpu.make_async_copy(ens.at[:, :, 0], xv, load_sem)
-    load.start()
     tile_row = pl.multiple_of((me // 8) * 8, 8)
     obs_load = pltpu.make_async_copy(obs.at[:, 0, pl.ds(tile_row, 8)], ov, obs_sem)
     obs_load.start()
 
-    flags = [mask[m].astype(jnp.float32) for m in range(2)]
+    mask_load.wait()
+    flags = [mask_s[m].astype(jnp.float32) for m in range(2)]
     fills = [(1.0 - f) * BIG for f in flags]
     lane = lax.broadcasted_iota(jnp.int32, (8, LANES), 1)
-    load.wait()
-    for t in range(4):
-        rows = pl.ds(8 * t, 8)
+    copies = []
+    for k, dx in enumerate(BLOCKS):
+        loads[k].wait()
+        base = lax.rem(here["member_0"] + dx, 4) * (8 * S_STRIDE)
 
         def put(row, low, high):
-            start = 8 * t * S_STRIDE + 2 * row
+            start = base + 2 * row
             sbuf[pl.ds(start, 8, stride=S_STRIDE), :] = low
             sbuf[pl.ds(start + 1, 8, stride=S_STRIDE), :] = high
 
@@ -116,7 +136,7 @@
             for c in range(FULL + 1):
                 width = LANES if c < FULL else TAIL
                 pair = [
-                    xv[m, v, rows, pl.ds(c * LANES, width)] * flags[m] + fills[m] for m in range(2)
+                    xv[k, m, v, :, pl.ds(c * LANES, width)] * flags[m] + fills[m] for m in range(2)
                 ]
                 low, high = jnp.minimum(*pair), jnp.maximum(*pair)
                 if c < FULL:
@@ -130,24 +150,25 @@
             jnp.concatenate([p[1] for p in tails] + [rest], axis=1),
         )
 
-    pl.semaphore_wait(barrier, len(plane) + len(line))
-    for off in line:
+        if k == 0:
+            pl.semaphore_wait(barrier, len(plane) + len(LINE))
+        for off in PLANE[k]:
+            target = peer(off)
+            start = pl.multiple_of(member_of(target) * S_STRIDE, 8)
+            slot = len(copies)
+            copy = pltpu.make_async_remote_copy(
+                src_ref=sbuf.at[pl.ds(start, SENT)],
+                dst_ref=rbuf.at[pl.ds(slot * R_STRIDE, SENT)],
+                send_sem=send_sem,
+                recv_sem=recv_sem.at[slot],
+                device_id=target,
+                device_id_type=MESH_ID,
+            )
+            copy.start()
+            copies.append(copy)
+
+    for off in LINE:
         pl.semaphore_signal(ready_sem, inc=1, device_id=peer(off), device_id_type=MESH_ID)
-
-    copies = []
-    for i, off in enumerate(plane):
-        target = peer(off)
-        start = pl.multiple_of(member_of(target) * S_STRIDE, 8)
-        copy = pltpu.make_async_remote_copy(
-            src_ref=sbuf.at[pl.ds(start, SENT)],
-            dst_ref=rbuf.at[pl.ds(i * R_STRIDE, SENT)],
-            send_sem=send_sem,
-            recv_sem=recv_sem.at[i],
-            device_id=target,
-            device_id_type=MESH_ID,
-        )
-        copy.start()
-        copies.append(copy)
 
     own = pl.multiple_of(me * S_STRIDE, 8)
     rbuf[pl.ds(31 * R_STRIDE, S_STRIDE), :] = sbuf[pl.ds(own, S_STRIDE), :]
@@ -167,21 +188,41 @@
     angle = (90.0 - jnp.full((1, LANES), global_row) * 180.0 / (GRID_LAT - 1)) * math.pi / 180.0
     weight = jnp.cos(angle)
 
-    for copy in copies:
+    def rows_of(q, k):
+        return pl.ds((k // 2) * R_STRIDE + 16 * q + k % 2, 8, stride=2)
+
+    def presort(first, count):
+        stage = []
+        sort_pairs(0, count, stage)
+        stage = pruned(stage, count)
+
+        def column(q, carry):
+            vals = [rbuf[rows_of(q, first + k), :] for k in range(count)]
+            sort_into(vals, stage)
+            for k in range(count):
+                rbuf[rows_of(q, first + k), :] = vals[k]
+            return carry
+
+        lax.fori_loop(0, COLS, column, 0)
+
+    for copy in copies[:16]:
         copy.wait_recv()
-
-    pairs = []
-    sort_pairs(0, 64, pairs)
-    pairs = pruned(pairs, VALID)
+    presort(0, 32)
+    for copy in copies[16:24]:
+        copy.wait_recv()
+    presort(32, 16)
+    for copy in copies[24:]:
+        copy.wait_recv()
+
+    stage = []
+    sort_pairs(48, 16, stage)
+    merge_pairs(32, 32, 1, stage)
+    merge_pairs(0, 64, 1, stage)
+    stage = pruned(stage, VALID)
 
     def column(q, sums):
-        vals = [
-            rbuf[pl.ds((k // 2) * R_STRIDE + 16 * q + k % 2, 8, stride=2), :] for k in range(64)
-        ]
-        for i, j, want_low, want_high in pairs:
-            a, b = vals[i], vals[j]
-            vals[i] = jnp.minimum(a, b) if want_low else None
-            vals[j] = jnp.maximum(a, b) if want_high else None
+        vals = [rbuf[rows_of(q, k), :] for k in range(64)]
+        sort_into(vals, stage)
         truth = obuf[pl.ds(pl.multiple_of(8 * q, 8), 8), :]
         skill = [jnp.zeros((8, LANES), jnp.float32) for _ in range(2)]
         spread = [jnp.zeros((8, LANES), jnp.float32) for _ in range(2)]
@@ -214,8 +255,8 @@
     asend[0] = message
     abuf[my_id] = message
 
-    pl.semaphore_wait(ready_sem, len(line))
-    for off in everyone:
+    pl.semaphore_wait(ready_sem, len(LINE))
+    for off in EVERYONE:
         pltpu.make_async_remote_copy(
             src_ref=asend.at[0],
             dst_ref=abuf.at[my_id],
@@ -233,27 +274,34 @@
 
     sent = sbuf.at[pl.ds(0, len(plane) * SENT)]
     pltpu.make_async_copy(sent, sent, send_sem).wait()
-    arrived = abuf.at[pl.ds(0, len(everyone))]
+    arrived = abuf.at[pl.ds(0, len(EVERYONE))]
     pltpu.make_async_copy(arrived, arrived, arecv_sem).wait()
     total = jnp.sum(abuf[:, 0, :], axis=0, keepdims=True) * (1.0 / (4 * 32 * GRID_LON))
     score_out[...] = total
     pltpu.make_async_copy(arrived, arrived, asend_sem).wait()
 
 
+def write_kernel(crps, score, crps_out, score_out):
+    crps_out[...] = crps[...]
+    score_out[...] = score[:, :VARS]
+
+
 def on_device(ensemble, observation, valid_mask, band_start):
     vmem = pl.BlockSpec(memory_space=pltpu.VMEM)
+    hbm = pl.BlockSpec(memory_space=pltpu.HBM)
     smem = pl.BlockSpec(memory_space=pltpu.SMEM)
-    hbm = pl.BlockSpec(memory_space=pl.ANY)
+    in_hbm = [
+        pltpu.with_memory_space_constraint(a, pltpu.HBM)
+        for a in (ensemble, observation, valid_mask)
+    ]
+    field = jax.ShapeDtypeStruct((VARS, 1, 1, GRID_LON), jnp.float32)
     crps_field, score = pl.pallas_call(
         kernel,
-        out_shape=(
-            jax.ShapeDtypeStruct((VARS, 1, 1, GRID_LON), jnp.float32),
-            jax.ShapeDtypeStruct((1, LANES), jnp.float32),
-        ),
-        in_specs=[hbm, hbm, smem, smem],
+        out_shape=(field, jax.ShapeDtypeStruct((1, LANES), jnp.float32)),
+        in_specs=[hbm, hbm, hbm, smem],
         out_specs=(vmem, vmem),
         scratch_shapes=[
-            pltpu.VMEM((2, VARS, 32, GRID_LON), jnp.float32),
+            pltpu.VMEM((4, 2, VARS, 8, GRID_LON), jnp.float32),
             pltpu.VMEM((VARS, 8, GRID_LON), jnp.float32),
             pltpu.VMEM((32 * S_STRIDE, LANES), jnp.float32),
             pltpu.VMEM((32 * R_STRIDE, LANES), jnp.float32),
@@ -261,6 +309,8 @@
             pltpu.VMEM((8 * COLS, LANES), jnp.float32),
             pltpu.VMEM((1, 1, LANES), jnp.float32),
             pltpu.VMEM((128, 1, LANES), jnp.float32),
+            pltpu.SMEM((2,), jnp.int32),
+            pltpu.SemaphoreType.DMA((4,)),
             pltpu.SemaphoreType.DMA,
             pltpu.SemaphoreType.DMA,
             pltpu.SemaphoreType.DMA,
@@ -269,10 +319,20 @@
             pltpu.SemaphoreType.DMA,
             pltpu.SemaphoreType.REGULAR,
         ],
-        compiler_params=pltpu.CompilerParams(collective_id=0, has_side_effects=True),
+        compiler_params=pltpu.CompilerParams(
+            collective_id=0, has_side_effects=True, vmem_limit_bytes=8 * 1024 * 1024
+        ),
         name="crps",
-    )(ensemble, observation, valid_mask, band_start)
-    return crps_field, score[0, :VARS].reshape(VARS, 1)
+    )(*in_hbm, band_start)
+    crps_field, score = pl.pallas_call(
+        write_kernel,
+        out_shape=(field, jax.ShapeDtypeStruct((1, VARS), jnp.float32)),
+        in_specs=[vmem, vmem],
+        out_specs=(vmem, vmem),
+        compiler_params=pltpu.CompilerParams(vmem_limit_bytes=1024 * 1024),
+        name="write",
+    )(crps_field, score)
+    return crps_field, score.reshape(VARS, 1)
 
 
 def solution(mesh):

time: 35.4 us -> 32.2 us (0.910)
  local copies, waits for them, and re-layouts: 2.51 us -> 0 us
  Pallas kernels: 31.4 us -> 30.7 us
    unnamed x1 -> x0, local copies, waits for them, and re-layouts: 1.33 us -> none
    another operation x1 -> x0, local copies, waits for them, and re-layouts: 1.18 us -> none  [on_device(): return (crps_field, score[0, :VARS].reshape(VARS, 1))]
    pallas_call x1 -> x2, Pallas kernels: 31.4 us -> 30.7 us  [the longest x1 30.1 us: on_device(): pl.pallas_call(kernel, out_shape=(field, jax.ShapeDtypeStruct((1, LANES),...]
where the time goes in v2:
time: 32.2 us; the launch traced here: 32 us
  Pallas kernels  30.7 us (95%)
  between operations  1.28 us (4%)
    pallas_call x1, Pallas kernels, on_device(): pl.pallas_call(kernel, out_shape=(field, jax.ShapeDtypeStruct((1, LANES),...  30.1 us

profile of v2, /device:TPU:1, one launch (start us, length us, event | category | flops | bytes accessed | tf_op | source)
XLA Modules:
  0.0 32.0 jit_solution(5738190149155488765)
XLA Ops:
  1.3 30.1 %crps.1 = (f32[3,1,1,1440]{3,2,1,0:T(1,128)S(1)}, f32[1,128]{1,0:T(1,128)S(1)}) custom-call(f32[2,3,1,32,1440]{4,3,2,1,0:T(8,128)} %ens.1, f32[3,1,32,1440]{3,2,1,0:T(8,128)} %obs.1, s32[2]{0:T(128)} %mask.1, s32[1]{0:T(128)S(6)} %copy.6.band), custom_call_target="tpu_custom_call" | custom-call | tf_op jit(solution)/shard_map/crps/pallas_call | solution.py:298
  31.4 0.6 %write.1 = (f32[3,1,1,1440]{3,2,1,0:T(1,128)}, f32[1,3]{1,0:T(1,128)}) custom-call(f32[3,1,1,1440]{3,2,1,0:T(1,128)S(1)} %get-tuple-element.6.crps, f32[1,128]{1,0:T(1,128)S(1)} %get-tuple-element.7.score), custom_call_target="tpu_custom_call" | custom-call | tf_op jit(solution)/shard_map/write/pallas_call | solution.py:327

commit v3 on v2

--- a/solution.py
+++ b/solution.py
@@ -42,6 +42,10 @@
     return sorted(found, key=lambda o: -hops(o))
 
 
+def chip_hops(o):
+    return sum(min(o[a], SIZES[a] - o[a]) for a in ("member_0", "member_1"))
+
+
 def peer(offset):
     return {a: lax.rem(lax.axis_index(a) + offset.get(a, 0), SIZES[a]) for a in AXES}
 
@@ -78,8 +82,16 @@
     return kept[::-1]
 
 
-BLOCKS = (2, 1, 3, 0)
-PLANE = [[o for o in offsets(MEMBER) if o["member_0"] == dx] for dx in BLOCKS]
+BLOCKS = (1, 3, 0, 2)
+LEVELS = 2
+PLANE = offsets(MEMBER)
+NEAR = [o for o in PLANE if o["member_0"] == 0 or o["member_1"] == 0]
+SIDE = [o for o in NEAR if o["member_1"] == 0 and o["member_2"] == 0]
+FAR = [o for o in PLANE if o not in NEAR]
+ROUNDS = (
+    [o for o in NEAR if chip_hops(o) == 1],
+    FAR + [o for o in NEAR if chip_hops(o) == 2] + [o for o in NEAR if chip_hops(o) == 0],
+)
 LINE = offsets(("lat",))
 EVERYONE = offsets(AXES)
 
@@ -94,7 +106,7 @@
 def kernel(
     ens, obs, mask, band, crps_out, score_out,
     xv, ov, sbuf, rbuf, obuf, cbuf, asend, abuf, mask_s,
-    load_sem, obs_sem, flag_sem, send_sem, recv_sem, asend_sem, arecv_sem, ready_sem,
+    load_sem, obs_sem, flag_sem, send_sem, recv_sem, asend_sem, arecv_sem, ready_sem, hop_sem,
 ):
     here = {a: lax.axis_index(a) for a in AXES}
     me = member_of(here)
@@ -109,19 +121,26 @@
         loads.append(load)
 
     barrier = pltpu.get_barrier_semaphore()
-    plane = [o for block in PLANE for o in block]
-    for off in offsets(MEMBER) + LINE:
+    for off in NEAR + LINE:
         pl.semaphore_signal(barrier, inc=1, device_id=peer(off), device_id_type=MESH_ID)
 
     tile_row = pl.multiple_of((me // 8) * 8, 8)
     obs_load = pltpu.make_async_copy(obs.at[:, 0, pl.ds(tile_row, 8)], ov, obs_sem)
     obs_load.start()
 
+    pl.semaphore_wait(barrier, len(NEAR) + len(LINE))
+
+    def pass_on(level):
+        for off in SIDE:
+            pl.semaphore_signal(
+                hop_sem.at[level], inc=1, device_id=peer(off), device_id_type=MESH_ID
+            )
+
+    pass_on(0)
     mask_load.wait()
     flags = [mask_s[m].astype(jnp.float32) for m in range(2)]
     fills = [(1.0 - f) * BIG for f in flags]
     lane = lax.broadcasted_iota(jnp.int32, (8, LANES), 1)
-    copies = []
     for k, dx in enumerate(BLOCKS):
         loads[k].wait()
         base = lax.rem(here["member_0"] + dx, 4) * (8 * S_STRIDE)
@@ -150,15 +169,21 @@
             jnp.concatenate([p[1] for p in tails] + [rest], axis=1),
         )
 
-        if k == 0:
-            pl.semaphore_wait(barrier, len(plane) + len(LINE))
-        for off in PLANE[k]:
+    own = pl.multiple_of(me * S_STRIDE, 8)
+    rbuf[pl.ds(0, S_STRIDE), :] = sbuf[pl.ds(own, S_STRIDE), :]
+    copies = []
+    for level, group in enumerate(ROUNDS):
+        if level > 0:
+            pl.semaphore_wait(hop_sem.at[level - 1], len(SIDE))
+            if level < LEVELS - 1:
+                pass_on(level)
+        for off in group:
             target = peer(off)
             start = pl.multiple_of(member_of(target) * S_STRIDE, 8)
             slot = len(copies)
             copy = pltpu.make_async_remote_copy(
                 src_ref=sbuf.at[pl.ds(start, SENT)],
-                dst_ref=rbuf.at[pl.ds(slot * R_STRIDE, SENT)],
+                dst_ref=rbuf.at[pl.ds((slot + 1) * R_STRIDE, SENT)],
                 send_sem=send_sem,
                 recv_sem=recv_sem.at[slot],
                 device_id=target,
@@ -170,8 +195,6 @@
     for off in LINE:
         pl.semaphore_signal(ready_sem, inc=1, device_id=peer(off), device_id_type=MESH_ID)
 
-    own = pl.multiple_of(me * S_STRIDE, 8)
-    rbuf[pl.ds(31 * R_STRIDE, S_STRIDE), :] = sbuf[pl.ds(own, S_STRIDE), :]
     obs_load.wait()
     sub = lax.broadcasted_iota(jnp.int32, (8, LANES), 0)
     chosen = sub == lax.rem(me, 8)
@@ -205,13 +228,13 @@
 
         lax.fori_loop(0, COLS, column, 0)
 
-    for copy in copies[:16]:
+    for copy in copies[:15]:
         copy.wait_recv()
     presort(0, 32)
-    for copy in copies[16:24]:
+    for copy in copies[15:23]:
         copy.wait_recv()
     presort(32, 16)
-    for copy in copies[24:]:
+    for copy in copies[23:]:
         copy.wait_recv()
 
     stage = []
@@ -272,7 +295,7 @@
         last = cbuf[pl.ds(VARS * FULL, 1), :]
         crps_out[v, 0, :, pl.ds(FULL * LANES, TAIL)] = last[:, v * TAIL : (v + 1) * TAIL]
 
-    sent = sbuf.at[pl.ds(0, len(plane) * SENT)]
+    sent = sbuf.at[pl.ds(0, len(PLANE) * SENT)]
     pltpu.make_async_copy(sent, sent, send_sem).wait()
     arrived = abuf.at[pl.ds(0, len(EVERYONE))]
     pltpu.make_async_copy(arrived, arrived, arecv_sem).wait()
@@ -318,6 +341,7 @@
             pltpu.SemaphoreType.DMA,
             pltpu.SemaphoreType.DMA,
             pltpu.SemaphoreType.REGULAR,
+            pltpu.SemaphoreType.REGULAR((LEVELS - 1,)),
         ],
         compiler_params=pltpu.CompilerParams(
             collective_id=0, has_side_effects=True, vmem_limit_bytes=8 * 1024 * 1024

time: 32.2 us -> 31.6 us (0.981)
  Pallas kernels: 30.7 us -> 30.2 us
    pallas_call x1, Pallas kernels: 30.1 us -> 29.6 us  [on_device(): pl.pallas_call(kernel, out_shape=(field, jax.ShapeDtypeStruct((1, LANES),...]
where the time goes in v3:
time: 31.6 us; the launch traced here: 31.5 us
  Pallas kernels  30.2 us (96%)
  between operations  1.28 us (4%)
    pallas_call x1, Pallas kernels, on_device(): pl.pallas_call(kernel, out_shape=(field, jax.ShapeDtypeStruct((1, LANES),...  29.6 us

profile of v3, /device:TPU:1, one launch (start us, length us, event | category | flops | bytes accessed | tf_op | source)
XLA Modules:
  0.0 31.5 jit_solution(4453962968450665569)
XLA Ops:
  1.3 29.6 %crps.1 = (f32[3,1,1,1440]{3,2,1,0:T(1,128)S(1)}, f32[1,128]{1,0:T(1,128)S(1)}) custom-call(f32[2,3,1,32,1440]{4,3,2,1,0:T(8,128)} %ens.1, f32[3,1,32,1440]{3,2,1,0:T(8,128)} %obs.1, s32[2]{0:T(128)} %mask.1, s32[1]{0:T(128)S(6)} %copy.6.band), custom_call_target="tpu_custom_call" | custom-call | tf_op jit(solution)/shard_map/crps/pallas_call | solution.py:321
  30.8 0.6 %write.1 = (f32[3,1,1,1440]{3,2,1,0:T(1,128)}, f32[1,3]{1,0:T(1,128)}) custom-call(f32[3,1,1,1440]{3,2,1,0:T(1,128)S(1)} %get-tuple-element.6.crps, f32[1,128]{1,0:T(1,128)S(1)} %get-tuple-element.7.score), custom_call_target="tpu_custom_call" | custom-call | tf_op jit(solution)/shard_map/write/pallas_call | solution.py:351

commit v4 on v3

--- a/solution.py
+++ b/solution.py
@@ -88,10 +88,13 @@
 NEAR = [o for o in PLANE if o["member_0"] == 0 or o["member_1"] == 0]
 SIDE = [o for o in NEAR if o["member_1"] == 0 and o["member_2"] == 0]
 FAR = [o for o in PLANE if o not in NEAR]
-ROUNDS = (
-    [o for o in NEAR if chip_hops(o) == 1],
-    FAR + [o for o in NEAR if chip_hops(o) == 2] + [o for o in NEAR if chip_hops(o) == 0],
-)
+XY2 = [o for o in NEAR if chip_hops(o) == 2]
+C1 = [o for o in NEAR if chip_hops(o) == 0]
+D11 = [o for o in FAR if chip_hops(o) == 2]
+FARX = [o for o in FAR if chip_hops(o) > 2]
+ROUNDS = ([o for o in NEAR if chip_hops(o) == 1], FARX, D11 + XY2 + C1)
+RELAY = FAR[:2]
+SECOND = 1
 LINE = offsets(("lat",))
 EVERYONE = offsets(AXES)
 
@@ -106,7 +109,7 @@
 def kernel(
     ens, obs, mask, band, crps_out, score_out,
     xv, ov, sbuf, rbuf, obuf, cbuf, asend, abuf, mask_s,
-    load_sem, obs_sem, flag_sem, send_sem, recv_sem, asend_sem, arecv_sem, ready_sem, hop_sem,
+    load_sem, obs_sem, flag_sem, send_sem, recv_sem, relay_sem, asend_sem, arecv_sem, ready_sem, line_sem, hop_sem,
 ):
     here = {a: lax.axis_index(a) for a in AXES}
     me = member_of(here)
@@ -121,14 +124,27 @@
         loads.append(load)
 
     barrier = pltpu.get_barrier_semaphore()
-    for off in NEAR + LINE:
+    for off in NEAR:
         pl.semaphore_signal(barrier, inc=1, device_id=peer(off), device_id_type=MESH_ID)
+    last = here["lat"] // (SIZES["lat"] - 1)
+    late = here["lat"] // 2
+    mirror = SIZES["lat"] - 1 - here["lat"]
+
+    @pl.when(last == 0)
+    def _():
+        up = dict(here, lat=SIZES["lat"] - 1)
+        pl.semaphore_signal(barrier, inc=1, device_id=up, device_id_type=MESH_ID)
+
+    @pl.when(here["lat"] == 1)
+    def _():
+        up = dict(here, lat=2)
+        pl.semaphore_signal(barrier, inc=1, device_id=up, device_id_type=MESH_ID)
 
     tile_row = pl.multiple_of((me // 8) * 8, 8)
     obs_load = pltpu.make_async_copy(obs.at[:, 0, pl.ds(tile_row, 8)], ov, obs_sem)
     obs_load.start()
 
-    pl.semaphore_wait(barrier, len(NEAR) + len(LINE))
+    pl.semaphore_wait(barrier, len(NEAR) + len(LINE) * last + (late - last))
 
     def pass_on(level):
         for off in SIDE:
@@ -137,6 +153,11 @@
             )
 
     pass_on(0)
+
+    @pl.when(last == 1)
+    def _():
+        for off in LINE:
+            pl.semaphore_signal(line_sem, inc=1, device_id=peer(off), device_id_type=MESH_ID)
     mask_load.wait()
     flags = [mask_s[m].astype(jnp.float32) for m in range(2)]
     fills = [(1.0 - f) * BIG for f in flags]
@@ -171,26 +192,80 @@
 
     own = pl.multiple_of(me * S_STRIDE, 8)
     rbuf[pl.ds(0, S_STRIDE), :] = sbuf[pl.ds(own, S_STRIDE), :]
-    copies = []
+    slots = {}
+
+    def block(place):
+        return pl.ds(pl.multiple_of(place * R_STRIDE, 8), SENT)
+
+    def arrived_in(slot, place):
+        rows = rbuf.at[block(place)]
+        return pltpu.make_async_copy(rows, rows, recv_sem.at[slot])
+
+    def send(group):
+        for off in group:
+            target = peer(off)
+            start = pl.multiple_of(member_of(target) * S_STRIDE, 8)
+            slot = slots[str(off)]
+            place, flag = slot + 1, slot
+            if off in RELAY:
+                via = RELAY.index(off)
+                moved = late if via < SECOND else last
+                stop = dict(here, lat=mirror)
+                target = {a: target[a] * (1 - moved) + stop[a] * moved for a in AXES}
+                place = place * (1 - moved) + (32 + via) * moved
+                flag = flag * (1 - moved) + (31 + via) * moved
+            pltpu.make_async_remote_copy(
+                src_ref=sbuf.at[pl.ds(start, SENT)],
+                dst_ref=rbuf.at[block(place)],
+                send_sem=send_sem,
+                recv_sem=recv_sem.at[flag],
+                device_id=target,
+                device_id_type=MESH_ID,
+            ).start()
+
     for level, group in enumerate(ROUNDS):
-        if level > 0:
+        if level == 1:
             pl.semaphore_wait(hop_sem.at[level - 1], len(SIDE))
             if level < LEVELS - 1:
                 pass_on(level)
         for off in group:
-            target = peer(off)
-            start = pl.multiple_of(member_of(target) * S_STRIDE, 8)
-            slot = len(copies)
-            copy = pltpu.make_async_remote_copy(
-                src_ref=sbuf.at[pl.ds(start, SENT)],
-                dst_ref=rbuf.at[pl.ds((slot + 1) * R_STRIDE, SENT)],
-                send_sem=send_sem,
-                recv_sem=recv_sem.at[slot],
-                device_id=target,
-                device_id_type=MESH_ID,
-            )
-            copy.start()
-            copies.append(copy)
+            slots[str(off)] = len(slots)
+        if level < 2:
+            send(group)
+
+    early = 1 - late if SECOND else 1 - (here["lat"] + SIZES["lat"] - 1) // SIZES["lat"]
+
+    @pl.when(early == 0)
+    def _():
+        send(ROUNDS[2])
+
+    def forward(via):
+        arrived_in(31 + via, 32 + via).wait()
+        slot = slots[str(RELAY[via])]
+        pltpu.make_async_remote_copy(
+            src_ref=rbuf.at[block(32 + via)],
+            dst_ref=rbuf.at[block(slot + 1)],
+            send_sem=relay_sem.at[via],
+            recv_sem=recv_sem.at[slot],
+            device_id=dict(peer(RELAY[via]), lat=mirror),
+            device_id_type=MESH_ID,
+        ).start()
+
+    @pl.when(early == 1)
+    def _():
+        for via in range(SECOND):
+            forward(via)
+
+        @pl.when(here["lat"] == 0)
+        def _():
+            for via in range(SECOND, len(RELAY)):
+                forward(via)
+
+        send(ROUNDS[2])
+
+    @pl.when(last == 0)
+    def _():
+        pl.semaphore_wait(line_sem, 1)
 
     for off in LINE:
         pl.semaphore_signal(ready_sem, inc=1, device_id=peer(off), device_id_type=MESH_ID)
@@ -228,14 +303,14 @@
 
         lax.fori_loop(0, COLS, column, 0)
 
-    for copy in copies[:15]:
-        copy.wait_recv()
+    for slot in range(15):
+        arrived_in(slot, slot + 1).wait()
     presort(0, 32)
-    for copy in copies[15:23]:
-        copy.wait_recv()
+    for slot in range(15, 23):
+        arrived_in(slot, slot + 1).wait()
     presort(32, 16)
-    for copy in copies[23:]:
-        copy.wait_recv()
+    for slot in range(23, 31):
+        arrived_in(slot, slot + 1).wait()
 
     stage = []
     sort_pairs(48, 16, stage)
@@ -297,6 +372,13 @@
 
     sent = sbuf.at[pl.ds(0, len(PLANE) * SENT)]
     pltpu.make_async_copy(sent, sent, send_sem).wait()
+    relayed = rbuf.at[pl.ds(0, SENT)]
+    for via in range(len(RELAY)):
+
+        @pl.when(here["lat"] <= (1 if via < SECOND else 0))
+        def _():
+            pltpu.make_async_copy(relayed, relayed, relay_sem.at[via]).wait()
+
     arrived = abuf.at[pl.ds(0, len(EVERYONE))]
     pltpu.make_async_copy(arrived, arrived, arecv_sem).wait()
     total = jnp.sum(abuf[:, 0, :], axis=0, keepdims=True) * (1.0 / (4 * 32 * GRID_LON))
@@ -327,7 +409,7 @@
             pltpu.VMEM((4, 2, VARS, 8, GRID_LON), jnp.float32),
             pltpu.VMEM((VARS, 8, GRID_LON), jnp.float32),
             pltpu.VMEM((32 * S_STRIDE, LANES), jnp.float32),
-            pltpu.VMEM((32 * R_STRIDE, LANES), jnp.float32),
+            pltpu.VMEM(((32 + len(RELAY)) * R_STRIDE, LANES), jnp.float32),
             pltpu.VMEM((8 * COLS, LANES), jnp.float32),
             pltpu.VMEM((8 * COLS, LANES), jnp.float32),
             pltpu.VMEM((1, 1, LANES), jnp.float32),
@@ -337,9 +419,11 @@
             pltpu.SemaphoreType.DMA,
             pltpu.SemaphoreType.DMA,
             pltpu.SemaphoreType.DMA,
-            pltpu.SemaphoreType.DMA((31,)),
+            pltpu.SemaphoreType.DMA((31 + len(RELAY),)),
+            pltpu.SemaphoreType.DMA((len(RELAY),)),
             pltpu.SemaphoreType.DMA,
             pltpu.SemaphoreType.DMA,
+            pltpu.SemaphoreType.REGULAR,
             pltpu.SemaphoreType.REGULAR,
             pltpu.SemaphoreType.REGULAR((LEVELS - 1,)),
         ],

time: 31.6 us -> 31 us (0.981)
  Pallas kernels: 30.2 us -> 29.6 us
    pallas_call x1, Pallas kernels: 29.6 us -> 29 us  [on_device(): pl.pallas_call(kernel, out_shape=(field, jax.ShapeDtypeStruct((1, LANES),...]
where the time goes in v4:
time: 31 us; the launch traced here: 30.9 us
  Pallas kernels  29.6 us (95%)
  between operations  1.28 us (4%)
    pallas_call x1, Pallas kernels, on_device(): pl.pallas_call(kernel, out_shape=(field, jax.ShapeDtypeStruct((1, LANES),...  29 us

profile of v4, /device:TPU:1, one launch (start us, length us, event | category | flops | bytes accessed | tf_op | source)
XLA Modules:
  0.0 30.9 jit_solution(10646485458029131977)
XLA Ops:
  1.3 29.0 %crps.1 = (f32[3,1,1,1440]{3,2,1,0:T(1,128)S(1)}, f32[1,128]{1,0:T(1,128)S(1)}) custom-call(f32[2,3,1,32,1440]{4,3,2,1,0:T(8,128)} %ens.1, f32[3,1,32,1440]{3,2,1,0:T(8,128)} %obs.1, s32[2]{0:T(128)} %mask.1, s32[1]{0:T(128)S(6)} %copy.6.band), custom_call_target="tpu_custom_call" | custom-call | tf_op jit(solution)/shard_map/crps/pallas_call | solution.py:403
  30.3 0.6 %write.1 = (f32[3,1,1,1440]{3,2,1,0:T(1,128)}, f32[1,3]{1,0:T(1,128)}) custom-call(f32[3,1,1,1440]{3,2,1,0:T(1,128)S(1)} %get-tuple-element.6.crps, f32[1,128]{1,0:T(1,128)S(1)} %get-tuple-element.7.score), custom_call_target="tpu_custom_call" | custom-call | tf_op jit(solution)/shard_map/write/pallas_call | solution.py:435

commit v5 on v4

--- a/solution.py
+++ b/solution.py
@@ -54,26 +54,31 @@
     return (coords["member_0"] * 4 + coords["member_1"]) * 2 + coords["member_2"]
 
 
-def merge_pairs(lo, n, step, out):
-    jump = step * 2
-    if jump < n:
-        merge_pairs(lo, n, jump, out)
-        merge_pairs(lo + step, n, jump, out)
-        out.extend((i, i + step) for i in range(lo + step, lo + n - step, jump))
-    else:
-        out.append((lo, lo + step))
-
-
-def sort_pairs(lo, n, out):
-    if n > 2:
-        half = n // 2
-        sort_pairs(lo, half, out)
-        sort_pairs(lo + half, half, out)
-        merge_pairs(lo, n, 1, out)
+def merge_wires(a, b, out):
+    if not a or not b:
+        return a + b
+    if len(a) == 1 and len(b) == 1:
+        out.append((a[0], b[0]))
+        return [a[0], b[0]]
+    even = merge_wires(a[0::2], b[0::2], out)
+    odd = merge_wires(a[1::2], b[1::2], out)
+    merged = even[:1]
+    for i in range(max(len(odd), len(even) - 1)):
+        if i < len(odd) and i + 1 < len(even):
+            out.append((odd[i], even[i + 1]))
+        merged += odd[i : i + 1] + even[i + 1 : i + 2]
+    return merged
+
+
+def sort_wires(wires, out):
+    if len(wires) <= 2:
+        return wires
+    half = (len(wires) + 2) // 4 * 2
+    return merge_wires(sort_wires(wires[:half], out), sort_wires(wires[half:], out), out)
 
 
 def pruned(pairs, keep):
-    needed = set(range(keep))
+    needed = set(keep)
     kept = []
     for i, j in reversed(pairs):
         if i in needed or j in needed:
@@ -91,8 +96,12 @@
 XY2 = [o for o in NEAR if chip_hops(o) == 2]
 C1 = [o for o in NEAR if chip_hops(o) == 0]
 D11 = [o for o in FAR if chip_hops(o) == 2]
-FARX = [o for o in FAR if chip_hops(o) > 2]
-ROUNDS = ([o for o in NEAR if chip_hops(o) == 1], FARX, D11 + XY2 + C1)
+D3 = [o for o in FAR if chip_hops(o) == 3]
+D22 = [o for o in FAR if chip_hops(o) == 4]
+N1 = [o for o in NEAR if chip_hops(o) == 1]
+ROUNDS = (N1, C1 + D3 + D22, D11 + XY2)
+SLOTS = N1 + C1 + D3 + D11 + D22 + XY2
+GROUPS = (18, 8, 6)
 RELAY = FAR[:2]
 SECOND = 1
 LINE = offsets(("lat",))
@@ -229,7 +238,7 @@
             if level < LEVELS - 1:
                 pass_on(level)
         for off in group:
-            slots[str(off)] = len(slots)
+            slots[str(off)] = SLOTS.index(off)
         if level < 2:
             send(group)
 
@@ -289,34 +298,29 @@
     def rows_of(q, k):
         return pl.ds((k // 2) * R_STRIDE + 16 * q + k % 2, 8, stride=2)
 
-    def presort(first, count):
+    order, done = [], 0
+    for count in GROUPS:
+        for slot in range(max(done, 1), done + count):
+            arrived_in(slot - 1, slot).wait()
         stage = []
-        sort_pairs(0, count, stage)
-        stage = pruned(stage, count)
-
-        def column(q, carry):
-            vals = [rbuf[rows_of(q, first + k), :] for k in range(count)]
+        fresh = list(range(2 * done, 2 * (done + count)))
+        order = merge_wires(order, sort_wires(fresh, stage), stage)
+        done += count
+        if done == 32:
+            break
+        stage = pruned(stage, order)
+
+        def presort(q, carry, stage=stage, wires=range(2 * done)):
+            vals = [rbuf[rows_of(q, k), :] for k in wires]
             sort_into(vals, stage)
-            for k in range(count):
-                rbuf[rows_of(q, first + k), :] = vals[k]
+            for k in wires:
+                rbuf[rows_of(q, k), :] = vals[k]
             return carry
 
-        lax.fori_loop(0, COLS, column, 0)
-
-    for slot in range(15):
-        arrived_in(slot, slot + 1).wait()
-    presort(0, 32)
-    for slot in range(15, 23):
-        arrived_in(slot, slot + 1).wait()
-    presort(32, 16)
-    for slot in range(23, 31):
-        arrived_in(slot, slot + 1).wait()
-
-    stage = []
-    sort_pairs(48, 16, stage)
-    merge_pairs(32, 32, 1, stage)
-    merge_pairs(0, 64, 1, stage)
-    stage = pruned(stage, VALID)
+        lax.fori_loop(0, COLS, presort, 0)
+
+    order = order[:VALID]
+    stage = pruned(stage, order)
 
     def column(q, sums):
         vals = [rbuf[rows_of(q, k), :] for k in range(64)]
@@ -325,7 +329,7 @@
         skill = [jnp.zeros((8, LANES), jnp.float32) for _ in range(2)]
         spread = [jnp.zeros((8, LANES), jnp.float32) for _ in range(2)]
         for k in range(VALID // 2):
-            low, high = vals[k], vals[VALID - 1 - k]
+            low, high = vals[order[k]], vals[order[VALID - 1 - k]]
             skill[0] = skill[0] + jnp.abs(low - truth)
             skill[1] = skill[1] + jnp.abs(high - truth)
             spread[k % 2] = spread[k % 2] + (high - low) * float(VALID - 1 - 2 * k)

time: 31 us -> 30.6 us (0.987)
  Pallas kernels: 29.6 us -> 29.2 us
    pallas_call x1, Pallas kernels: 29 us -> 28.6 us  [on_device(): pl.pallas_call(kernel, out_shape=(field, jax.ShapeDtypeStruct((1, LANES),...]
where the time goes in v5:
time: 30.6 us; the launch traced here: 30.5 us
  Pallas kernels  29.2 us (95%)
  between operations  1.28 us (4%)
    pallas_call x1, Pallas kernels, on_device(): pl.pallas_call(kernel, out_shape=(field, jax.ShapeDtypeStruct((1, LANES),...  28.6 us

profile of v5, /device:TPU:1, one launch (start us, length us, event | category | flops | bytes accessed | tf_op | source)
XLA Modules:
  0.0 30.5 jit_solution(16080809484835104305)
XLA Ops:
  1.3 28.6 %crps.1 = (f32[3,1,1,1440]{3,2,1,0:T(1,128)S(1)}, f32[1,128]{1,0:T(1,128)S(1)}) custom-call(f32[2,3,1,32,1440]{4,3,2,1,0:T(8,128)} %ens.1, f32[3,1,32,1440]{3,2,1,0:T(8,128)} %obs.1, s32[2]{0:T(128)} %mask.1, s32[1]{0:T(128)S(6)} %copy.6.band), custom_call_target="tpu_custom_call" | custom-call | tf_op jit(solution)/shard_map/crps/pallas_call | solution.py:407
  29.8 0.6 %write.1 = (f32[3,1,1,1440]{3,2,1,0:T(1,128)}, f32[1,3]{1,0:T(1,128)}) custom-call(f32[3,1,1,1440]{3,2,1,0:T(1,128)S(1)} %get-tuple-element.6.crps, f32[1,128]{1,0:T(1,128)S(1)} %get-tuple-element.7.score), custom_call_target="tpu_custom_call" | custom-call | tf_op jit(solution)/shard_map/write/pallas_call | solution.py:439

commit v6 on v5

--- a/solution.py
+++ b/solution.py
@@ -44,6 +44,10 @@
 
 def chip_hops(o):
     return sum(min(o[a], SIZES[a] - o[a]) for a in ("member_0", "member_1"))
+
+
+def group_of(place):
+    return 0 if place < GROUPS[0] else 1 if place < GROUPS[0] + GROUPS[1] else 2
 
 
 def peer(offset):
@@ -125,12 +129,10 @@
 
     mask_load = pltpu.make_async_copy(mask, mask_s, flag_sem)
     mask_load.start()
-    loads = []
     for k, dx in enumerate(BLOCKS):
         first = pl.multiple_of(lax.rem(here["member_0"] + dx, 4) * 8, 8)
-        load = pltpu.make_async_copy(ens.at[:, :, 0, pl.ds(first, 8)], xv.at[k], load_sem.at[k])
+        load = pltpu.make_async_copy(ens.at[:, :, 0, pl.ds(first, 8)], xv.at[k], load_sem)
         load.start()
-        loads.append(load)
 
     barrier = pltpu.get_barrier_semaphore()
     for off in NEAR:
@@ -168,11 +170,11 @@
         for off in LINE:
             pl.semaphore_signal(line_sem, inc=1, device_id=peer(off), device_id_type=MESH_ID)
     mask_load.wait()
+    pltpu.make_async_copy(xv, xv, load_sem).wait()
     flags = [mask_s[m].astype(jnp.float32) for m in range(2)]
     fills = [(1.0 - f) * BIG for f in flags]
     lane = lax.broadcasted_iota(jnp.int32, (8, LANES), 1)
     for k, dx in enumerate(BLOCKS):
-        loads[k].wait()
         base = lax.rem(here["member_0"] + dx, 4) * (8 * S_STRIDE)
 
         def put(row, low, high):
@@ -206,23 +208,23 @@
     def block(place):
         return pl.ds(pl.multiple_of(place * R_STRIDE, 8), SENT)
 
-    def arrived_in(slot, place):
-        rows = rbuf.at[block(place)]
-        return pltpu.make_async_copy(rows, rows, recv_sem.at[slot])
+    def await_slots(flag, count):
+        rows = rbuf.at[pl.ds(0, count * SENT)]
+        pltpu.make_async_copy(rows, rows, recv_sem.at[flag]).wait()
 
     def send(group):
         for off in group:
             target = peer(off)
             start = pl.multiple_of(member_of(target) * S_STRIDE, 8)
             slot = slots[str(off)]
-            place, flag = slot + 1, slot
+            place, flag = slot + 1, group_of(slot + 1)
             if off in RELAY:
                 via = RELAY.index(off)
                 moved = late if via < SECOND else last
                 stop = dict(here, lat=mirror)
                 target = {a: target[a] * (1 - moved) + stop[a] * moved for a in AXES}
                 place = place * (1 - moved) + (32 + via) * moved
-                flag = flag * (1 - moved) + (31 + via) * moved
+                flag = flag * (1 - moved) + (len(GROUPS) + via) * moved
             pltpu.make_async_remote_copy(
                 src_ref=sbuf.at[pl.ds(start, SENT)],
                 dst_ref=rbuf.at[block(place)],
@@ -249,13 +251,13 @@
         send(ROUNDS[2])
 
     def forward(via):
-        arrived_in(31 + via, 32 + via).wait()
+        await_slots(len(GROUPS) + via, 1)
         slot = slots[str(RELAY[via])]
         pltpu.make_async_remote_copy(
             src_ref=rbuf.at[block(32 + via)],
             dst_ref=rbuf.at[block(slot + 1)],
             send_sem=relay_sem.at[via],
-            recv_sem=recv_sem.at[slot],
+            recv_sem=recv_sem.at[group_of(slot + 1)],
             device_id=dict(peer(RELAY[via]), lat=mirror),
             device_id_type=MESH_ID,
         ).start()
@@ -299,9 +301,8 @@
         return pl.ds((k // 2) * R_STRIDE + 16 * q + k % 2, 8, stride=2)
 
     order, done = [], 0
-    for count in GROUPS:
-        for slot in range(max(done, 1), done + count):
-            arrived_in(slot - 1, slot).wait()
+    for flag, count in enumerate(GROUPS):
+        await_slots(flag, count if done else count - 1)
         stage = []
         fresh = list(range(2 * done, 2 * (done + count)))
         order = merge_wires(order, sort_wires(fresh, stage), stage)
@@ -419,11 +420,11 @@
             pltpu.VMEM((1, 1, LANES), jnp.float32),
             pltpu.VMEM((128, 1, LANES), jnp.float32),
             pltpu.SMEM((2,), jnp.int32),
-            pltpu.SemaphoreType.DMA((4,)),
-            pltpu.SemaphoreType.DMA,
-            pltpu.SemaphoreType.DMA,
-            pltpu.SemaphoreType.DMA,
-            pltpu.SemaphoreType.DMA((31 + len(RELAY),)),
+            pltpu.SemaphoreType.DMA,
+            pltpu.SemaphoreType.DMA,
+            pltpu.SemaphoreType.DMA,
+            pltpu.SemaphoreType.DMA,
+            pltpu.SemaphoreType.DMA((len(GROUPS) + len(RELAY),)),
             pltpu.SemaphoreType.DMA((len(RELAY),)),
             pltpu.SemaphoreType.DMA,
             pltpu.SemaphoreType.DMA,

time: 30.6 us -> 30.3 us (level)
  no operation moved by 1% of the time
where the time goes in v6:
time: 30.3 us; the launch traced here: 30.2 us
  Pallas kernels  28.9 us (95%)
  between operations  1.28 us (4%)
    pallas_call x1, Pallas kernels, on_device(): pl.pallas_call(kernel, out_shape=(field, jax.ShapeDtypeStruct((1, LANES),...  28.3 us
    pallas_call x1, Pallas kernels, on_device(): pl.pallas_call(write_kernel, out_shape=(field, jax.ShapeDtypeStruct((1, V...  0.61 us

profile of v6, /device:TPU:1, one launch (start us, length us, event | category | flops | bytes accessed | tf_op | source)
XLA Modules:
  0.0 30.2 jit_solution(2690832263951694323)
XLA Ops:
  1.3 28.3 %crps.1 = (f32[3,1,1,1440]{3,2,1,0:T(1,128)S(1)}, f32[1,128]{1,0:T(1,128)S(1)}) custom-call(f32[2,3,1,32,1440]{4,3,2,1,0:T(8,128)} %ens.1, f32[3,1,32,1440]{3,2,1,0:T(8,128)} %obs.1, s32[2]{0:T(128)} %mask.1, s32[1]{0:T(128)S(6)} %copy.6.band), custom_call_target="tpu_custom_call" | custom-call | tf_op jit(solution)/shard_map/crps/pallas_call | solution.py:408
  29.6 0.6 %write.1 = (f32[3,1,1,1440]{3,2,1,0:T(1,128)}, f32[1,3]{1,0:T(1,128)}) custom-call(f32[3,1,1,1440]{3,2,1,0:T(1,128)S(1)} %get-tuple-element.6.crps, f32[1,128]{1,0:T(1,128)S(1)} %get-tuple-element.7.score), custom_call_target="tpu_custom_call" | custom-call | tf_op jit(solution)/shard_map/write/pallas_call | solution.py:440

commit v7 on v6

--- a/solution.py
+++ b/solution.py
@@ -359,13 +359,14 @@
     abuf[my_id] = message
 
     pl.semaphore_wait(ready_sem, len(LINE))
-    for off in EVERYONE:
+    targets = [dict(peer(off), lat=z) for z in range(SIZES["lat"]) for off in PLANE]
+    for target in targets + [peer(off) for off in LINE]:
         pltpu.make_async_remote_copy(
             src_ref=asend.at[0],
             dst_ref=abuf.at[my_id],
             send_sem=asend_sem,
             recv_sem=arecv_sem,
-            device_id=peer(off),
+            device_id=target,
             device_id_type=MESH_ID,
         ).start()
 

time: 30.3 us -> 30.2 us (level)
  no operation moved by 1% of the time
where the time goes in v7:
time: 30.2 us; the launch traced here: 30.1 us
  Pallas kernels  28.8 us (95%)
  between operations  1.28 us (4%)
    pallas_call x1, Pallas kernels, on_device(): pl.pallas_call(kernel, out_shape=(field, jax.ShapeDtypeStruct((1, LANES),...  28.2 us
    pallas_call x1, Pallas kernels, on_device(): pl.pallas_call(write_kernel, out_shape=(field, jax.ShapeDtypeStruct((1, V...  0.61 us

profile of v7, /device:TPU:1, one launch (start us, length us, event | category | flops | bytes accessed | tf_op | source)
XLA Modules:
  0.0 30.1 jit_solution(11751086017246838913)
XLA Ops:
  1.3 28.2 %crps.1 = (f32[3,1,1,1440]{3,2,1,0:T(1,128)S(1)}, f32[1,128]{1,0:T(1,128)S(1)}) custom-call(f32[2,3,1,32,1440]{4,3,2,1,0:T(8,128)} %ens.1, f32[3,1,32,1440]{3,2,1,0:T(8,128)} %obs.1, s32[2]{0:T(128)} %mask.1, s32[1]{0:T(128)S(6)} %copy.6.band), custom_call_target="tpu_custom_call" | custom-call | tf_op jit(solution)/shard_map/crps/pallas_call | solution.py:409
  29.5 0.6 %write.1 = (f32[3,1,1,1440]{3,2,1,0:T(1,128)}, f32[1,3]{1,0:T(1,128)}) custom-call(f32[3,1,1,1440]{3,2,1,0:T(1,128)S(1)} %get-tuple-element.6.crps, f32[1,128]{1,0:T(1,128)S(1)} %get-tuple-element.7.score), custom_call_target="tpu_custom_call" | custom-call | tf_op jit(solution)/shard_map/write/pallas_call | solution.py:441

commit v8 on v7

--- a/solution.py
+++ b/solution.py
@@ -347,7 +347,7 @@
         return tuple(result)
 
     sums = lax.fori_loop(
-        0, COLS, column, tuple(jnp.zeros((8, LANES), jnp.float32) for _ in range(VARS))
+        0, COLS, column, tuple(jnp.zeros((8, LANES), jnp.float32) for _ in range(VARS)), unroll=True
     )
     totals = [jnp.sum(s, axis=(0, 1), keepdims=True) for s in sums]
     one_lane = lax.broadcasted_iota(jnp.int32, (1, LANES), 1)

time: 30.2 us -> 30.2 us (level)
  no operation moved by 1% of the time
where the time goes in v8:
time: 30.2 us; the launch traced here: 30 us
  Pallas kernels  28.7 us (95%)
  between operations  1.28 us (4%)
    pallas_call x1, Pallas kernels, on_device(): pl.pallas_call(kernel, out_shape=(field, jax.ShapeDtypeStruct((1, LANES),...  28.1 us
    pallas_call x1, Pallas kernels, on_device(): pl.pallas_call(write_kernel, out_shape=(field, jax.ShapeDtypeStruct((1, V...  0.61 us

profile of v8, /device:TPU:1, one launch (start us, length us, event | category | flops | bytes accessed | tf_op | source)
XLA Modules:
  0.0 30.0 jit_solution(6547545532383006390)
XLA Ops:
  1.3 28.1 %crps.1 = (f32[3,1,1,1440]{3,2,1,0:T(1,128)S(1)}, f32[1,128]{1,0:T(1,128)S(1)}) custom-call(f32[2,3,1,32,1440]{4,3,2,1,0:T(8,128)} %ens.1, f32[3,1,32,1440]{3,2,1,0:T(8,128)} %obs.1, s32[2]{0:T(128)} %mask.1, s32[1]{0:T(128)S(6)} %copy.6.band), custom_call_target="tpu_custom_call" | custom-call | tf_op jit(solution)/shard_map/crps/pallas_call | solution.py:409
  29.4 0.6 %write.1 = (f32[3,1,1,1440]{3,2,1,0:T(1,128)}, f32[1,3]{1,0:T(1,128)}) custom-call(f32[3,1,1,1440]{3,2,1,0:T(1,128)S(1)} %get-tuple-element.6.crps, f32[1,128]{1,0:T(1,128)S(1)} %get-tuple-element.7.score), custom_call_target="tpu_custom_call" | custom-call | tf_op jit(solution)/shard_map/write/pallas_call | solution.py:441

commit v9 on v7

--- a/solution.py
+++ b/solution.py
@@ -105,7 +105,7 @@
 N1 = [o for o in NEAR if chip_hops(o) == 1]
 ROUNDS = (N1, C1 + D3 + D22, D11 + XY2)
 SLOTS = N1 + C1 + D3 + D11 + D22 + XY2
-GROUPS = (18, 8, 6)
+GROUPS = (16, 10, 6)
 RELAY = FAR[:2]
 SECOND = 1
 LINE = offsets(("lat",))

time: 30.2 us -> 30.2 us (level)
  no operation moved by 1% of the time
where the time goes in v9:
time: 30.2 us; the launch traced here: 30.1 us
  Pallas kernels  28.8 us (95%)
  between operations  1.28 us (4%)
    pallas_call x1, Pallas kernels, on_device(): pl.pallas_call(kernel, out_shape=(field, jax.ShapeDtypeStruct((1, LANES),...  28.2 us
    pallas_call x1, Pallas kernels, on_device(): pl.pallas_call(write_kernel, out_shape=(field, jax.ShapeDtypeStruct((1, V...  0.61 us

profile of v9, /device:TPU:1, one launch (start us, length us, event | category | flops | bytes accessed | tf_op | source)
XLA Modules:
  0.0 30.1 jit_solution(6102998375787865279)
XLA Ops:
  1.3 28.2 %crps.1 = (f32[3,1,1,1440]{3,2,1,0:T(1,128)S(1)}, f32[1,128]{1,0:T(1,128)S(1)}) custom-call(f32[2,3,1,32,1440]{4,3,2,1,0:T(8,128)} %ens.1, f32[3,1,32,1440]{3,2,1,0:T(8,128)} %obs.1, s32[2]{0:T(128)} %mask.1, s32[1]{0:T(128)S(6)} %copy.6.band), custom_call_target="tpu_custom_call" | custom-call | tf_op jit(solution)/shard_map/crps/pallas_call | solution.py:409
  29.5 0.6 %write.1 = (f32[3,1,1,1440]{3,2,1,0:T(1,128)}, f32[1,3]{1,0:T(1,128)}) custom-call(f32[3,1,1,1440]{3,2,1,0:T(1,128)S(1)} %get-tuple-element.6.crps, f32[1,128]{1,0:T(1,128)S(1)} %get-tuple-element.7.score), custom_call_target="tpu_custom_call" | custom-call | tf_op jit(solution)/shard_map/write/pallas_call | solution.py:441
